TPU v7x, 32 devices: a whole 2x2x4 slice. The times are simulated.
32 devices in a mesh: groups: 2 (over y), blk: 4 (over z), ulysses: 2 (over x), cfg: 2 (over core).
Axes of the slice: x: 2, y: 2, z: 4, core: 2. Of those that a mesh axis runs over, the one named last changes fastest.
Arguments:
- img_tokens: bfloat16 [2, 2, 512, 2432], P('cfg', 'groups', ('blk', 'ulysses')), parts along dimension 1, may hold values from -72 to 72
- text_tokens: bfloat16 [2, 2, 48, 2432], P('cfg', 'groups', ('blk', 'ulysses')), parts along dimension 1, may hold values from -6 to 6
- text_lengths: int32 [2, 2], P('cfg', 'groups'), parts along dimension 1, may hold values from 12 to 48
- timestep: int32 [2], P('groups'), parts along dimension 0, may hold values from 0 to 999
- pooled: float32 [2, 2, 2432], P(None, 'groups'), parts along dimension 1, may hold values from -6 to 6
- time_weight: bfloat16 [256, 2432], replicated, may hold values from -0.375 to 0.375
- time_second: bfloat16 [2432, 2432], P(None, ('blk', 'ulysses', 'cfg')), may hold values from -0.125 to 0.125
- mod_weight: bfloat16 [2432, 24320], P(None, ('blk', 'ulysses', 'cfg')), may hold values from -0.125 to 0.125
- proj_weight: bfloat16 [5, 2432, 2048], P(None, None, ('ulysses', 'cfg')), may hold values from -0.125 to 0.125
- out_weight: bfloat16 [2048, 2432], P(('ulysses', 'cfg')), may hold values from -0.125 to 0.125
- expand_weight: bfloat16 [2432, 7168], P('blk', ('ulysses', 'cfg')), may hold values from -0.125 to 0.125
- reduce_weight: bfloat16 [7168, 2432], P(('ulysses', 'cfg'), 'blk'), may hold values from -0.0625 to 0.0625
- qk_gain: float32 [3, 64], replicated, may hold values from 0.5 to 10
- final_weight: bfloat16 [2432, 64], replicated, may hold values from -0.125 to 0.125
Outputs:
- guided: float32 [2, 16, 16, 128], P('groups', None, ('blk', 'ulysses', 'cfg')), parts along dimension 0
There are 2 independent parts, one for each index of `groups`. A program takes and returns all parts, laid end to end along the dimension named above; an argument that names none is the same for every part. Nothing has to cross between parts.
All inputs are finite; a program needn't handle non-finite values.
Results may differ from a plain program's by a relative error of at most 0.011.
The roundings to bfloat16 on the way count: a program that leaves them out, or rounds other values in their place, can miss the bound.
Values may be sent and summed in bfloat16 or wider, within the bound.
A program may use at most 192 MiB of HBM per device.

v0:
```python
import math
import jax
import jax.numpy as jnp
from jax import lax
from jax.sharding import PartitionSpec as P

GUIDANCE = 3.5
LN_EPS = 1e-06
RMS_EPS = 1e-06
NEG_FILL = -1e30
block_keys = 512


def from_partner(value, axis, stride):
    mask = 2**stride
    pairs = [(source, source ^ mask) for source in range(lax.axis_size(axis))]
    return lax.ppermute(value, axis, pairs)


def sinusoid(timestep, feature_count):
    half_width = feature_count // 2
    frequency = jnp.exp(-math.log(10000.0) * jnp.arange(half_width, dtype=jnp.float32) / half_width)
    angles = timestep.astype(jnp.float32)[:, None] * frequency[None, :]
    return jnp.concatenate([jnp.cos(angles), jnp.sin(angles)], axis=1)


def layer_norm(values):
    average = jnp.mean(values, axis=-1, keepdims=True)
    centred = values - average
    variance = jnp.mean(centred * centred, axis=-1, keepdims=True)
    return centred * lax.rsqrt(variance + LN_EPS)


def modulate(values, shift, scale):
    return (layer_norm(values.astype(jnp.float32)) * (1.0 + scale) + shift).astype(jnp.bfloat16)


def rms_heads(values, gain):
    head_size = gain.shape[0]
    shaped = values.reshape(values.shape[:-1] + (values.shape[-1] // head_size, head_size))
    inverse = lax.rsqrt(jnp.mean(shaped * shaped, axis=-1, keepdims=True) + RMS_EPS)
    return (shaped * inverse * gain).reshape(values.shape).astype(jnp.bfloat16)


def finish(img_proj, txt_proj, gain_rows):
    img_set = jnp.stack(
        [
            rms_heads(img_proj[0], gain_rows[0]),
            rms_heads(img_proj[1], gain_rows[1]),
            img_proj[2].astype(jnp.bfloat16),
        ]
    )
    txt_set = jnp.stack([rms_heads(txt_proj[0], gain_rows[2]), txt_proj[1].astype(jnp.bfloat16)])
    return (img_set, txt_set)


def attend(state_now, query_heads, key_rows, value_rows, usable, scale):
    running_max, running_total, running_sum = state_now
    prompts, query_count, head_count, head_size = query_heads.shape
    key_count = key_rows.shape[1]
    key_heads = key_rows.reshape(prompts, key_count, head_count, head_size)
    value_heads = value_rows.reshape(prompts, key_count, head_count, head_size)
    scores = (
        jnp.einsum("pqhd,pkhd->phqk", query_heads, key_heads, preferred_element_type=jnp.float32)
        * scale
    )
    allowed = usable[:, None, None, :]
    block_max = jnp.max(jnp.where(allowed, scores, NEG_FILL), axis=3)
    new_max = jnp.maximum(running_max, block_max)
    weights = jnp.where(allowed, jnp.exp(scores - new_max[..., None]), 0.0)
    factor = jnp.exp(running_max - new_max)
    running_total = running_total * factor + jnp.sum(weights, axis=3)
    update = jnp.einsum(
        "phqk,pkhd->pqhd",
        weights.astype(jnp.bfloat16),
        value_heads,
        preferred_element_type=jnp.float32,
    )
    running_sum = running_sum * factor.transpose(0, 2, 1)[..., None] + update
    return (new_max, running_total, running_sum)


def attend_rows(state_now, query_heads, key_value, usable, scale):
    key_count = key_value.shape[2]
    for first_key in range(0, key_count, block_keys):
        last_key = min(first_key + block_keys, key_count)
        state_now = attend(
            state_now,
            query_heads,
            key_value[0, :, first_key:last_key],
            key_value[1, :, first_key:last_key],
            usable[:, first_key:last_key],
            scale,
        )
    return state_now


def make_fold(query_heads, lengths, img_span, txt_span, scale):
    span = img_span + txt_span

    def fold(state_now, kv_piece, first_row):
        key_count = kv_piece.shape[2]
        positions = jnp.arange(key_count, dtype=jnp.int32)
        shard_index = positions // span
        offset = positions - shard_index * span
        text_slot = offset - img_span
        usable = (offset < img_span)[None, :] | (text_slot[None, :] < lengths[:, None])
        return attend_rows(state_now, query_heads, kv_piece, usable, scale)

    return fold


def body(
    img_tokens,
    text_tokens,
    text_lengths,
    timestep,
    pooled,
    time_weight,
    time_second,
    mod_weight,
    proj_weight,
    out_weight,
    expand_weight,
    reduce_weight,
    qk_gain,
    final_weight,
):
    model_width = img_tokens.shape[3]
    prompts = img_tokens.shape[1]
    head_size = qk_gain.shape[1]
    branch = lax.axis_index("cfg")
    sinusoid_rows = sinusoid(timestep, time_weight.shape[0]).astype(jnp.bfloat16)
    time_hidden = jax.nn.silu(
        jnp.dot(sinusoid_rows, time_weight, preferred_element_type=jnp.float32)
    ).astype(jnp.bfloat16)
    time_part = jnp.dot(time_hidden, time_second, preferred_element_type=jnp.float32)
    time_embed = lax.all_gather(time_part, ("blk", "ulysses", "cfg"), axis=1, tiled=True)
    acted = jax.nn.silu(time_embed[None] + pooled).astype(jnp.bfloat16)
    mod_part = jnp.einsum("bpd,dc->bpc", acted, mod_weight, preferred_element_type=jnp.float32)
    mod_all = lax.all_gather(mod_part, ("blk", "ulysses", "cfg"), axis=2, tiled=True)
    own_mod = lax.dynamic_index_in_dim(mod_all, branch, 0, keepdims=False).reshape(
        prompts, 10, model_width
    )
    image_rows = img_tokens[0]
    text_rows = text_tokens[0]
    lengths = text_lengths[0]
    h_img = modulate(image_rows, own_mod[:, 0:1], own_mod[:, 1:2])
    h_txt = modulate(text_rows, own_mod[:, 4:5], own_mod[:, 3:4])
    rows_img, rows_txt = (
        lax.all_gather(h_img, "ulysses", axis=1, tiled=True),
        lax.all_gather(h_txt, "ulysses", axis=1, tiled=True),
    )
    img_span = rows_img.shape[1]
    txt_span = rows_txt.shape[1]
    img_count = 3 * prompts * img_span
    weight_piece = lax.all_gather(proj_weight, "cfg", axis=2, tiled=True)
    columns = weight_piece.shape[2]
    img_part = jnp.einsum(
        "prd,jdc->jprc", rows_img, weight_piece[0:3], preferred_element_type=jnp.float32
    )
    txt_part = jnp.einsum(
        "prd,jdc->jprc", rows_txt, weight_piece[3:5], preferred_element_type=jnp.float32
    )
    stacked_rows = jnp.concatenate(
        [img_part.reshape(-1, columns), txt_part.reshape(-1, columns)], axis=0
    )
    img_proj = stacked_rows[:img_count].reshape(3, prompts, img_span, -1)
    txt_proj = stacked_rows[img_count:].reshape(2, prompts, txt_span, -1)
    img_set, txt_set = finish(img_proj, txt_proj, qk_gain)
    inner_local = img_set.shape[3]
    head_count = inner_local // head_size
    query_heads = img_set[0].reshape(prompts, img_span, head_count, head_size)
    scale = 1.0 / math.sqrt(head_size)
    start_state = (
        jnp.full((prompts, head_count, img_span), NEG_FILL, jnp.float32),
        jnp.zeros((prompts, head_count, img_span), jnp.float32),
        jnp.zeros((prompts, img_span, head_count, head_size), jnp.float32),
    )
    text_kv = lax.all_gather(jnp.stack([txt_set[0], txt_set[1]]), "blk", axis=2, tiled=True)
    slot_usable = jnp.arange(text_kv.shape[2], dtype=jnp.int32)[None, :] < lengths[:, None]
    text_state = attend_rows(start_state, query_heads, text_kv, slot_usable, scale)
    image_kv = jnp.stack([img_set[1], img_set[2]])
    fold = make_fold(query_heads, lengths, img_span, 0, scale)
    final_state = fold(
        text_state, lax.all_gather(image_kv, "blk", axis=2, tiled=True), jnp.int32(0)
    )
    running_max, running_total, running_sum = final_state
    mixed = (running_sum / running_total.transpose(0, 2, 1)[..., None]).astype(jnp.bfloat16)
    mixed_rows = mixed.reshape(prompts, img_span, inner_local).transpose(1, 0, 2)
    out_gathered = lax.all_gather(out_weight, "cfg", axis=0, tiled=True)
    token_count = image_rows.shape[1]
    segment = mixed_rows
    attended = lax.psum_scatter(
        jnp.einsum("rpc,cd->rpd", segment, out_gathered, preferred_element_type=jnp.float32).astype(
            jnp.bfloat16
        ),
        "ulysses",
        scatter_dimension=0,
        tiled=True,
    ).astype(jnp.float32)
    attended = attended.transpose(1, 0, 2)
    residual = image_rows.astype(jnp.float32) + own_mod[:, 2:3] * attended
    feed_input = modulate(residual, own_mod[:, 7:8], own_mod[:, 8:9]).reshape(
        prompts * token_count, model_width
    )
    feed_all = lax.all_gather(feed_input, ("ulysses", "cfg"), axis=0, tiled=True)
    columns = feed_all
    pre_active = jnp.dot(
        columns,
        lax.all_gather(expand_weight, "blk", axis=0, tiled=True),
        preferred_element_type=jnp.float32,
    )
    feed_hidden = jax.nn.gelu(pre_active, approximate=True).astype(jnp.bfloat16)
    reduce_full = lax.all_gather(reduce_weight, "blk", axis=1, tiled=True)
    segment = feed_hidden
    feed_out = lax.psum_scatter(
        jnp.dot(segment, reduce_full, preferred_element_type=jnp.float32).astype(jnp.bfloat16),
        ("ulysses", "cfg"),
        scatter_dimension=0,
        tiled=True,
    ).astype(jnp.float32)
    second_residual = residual + own_mod[:, 9:10] * feed_out.reshape(
        prompts, token_count, model_width
    )
    final_rows = modulate(second_residual, own_mod[:, 6:7], own_mod[:, 5:6])
    noise = jnp.einsum("prd,dc->prc", final_rows, final_weight, preferred_element_type=jnp.float32)
    latent_channels = final_weight.shape[1] // 4
    noise_own = noise.reshape(prompts, token_count, 2, 2, latent_channels).transpose(0, 4, 2, 1, 3)
    noise_own = noise_own.reshape(prompts, latent_channels, 2, 2 * token_count)
    kept_row = lax.dynamic_slice_in_dim(noise_own, branch, 1, 2)
    sent_row = lax.dynamic_slice_in_dim(noise_own, 1 - branch, 1, 2)
    noise_pair = from_partner(sent_row, "cfg", 0)
    noise_cond = jnp.where(branch == 0, kept_row, noise_pair)
    noise_uncond = jnp.where(branch == 0, noise_pair, kept_row)
    return noise_uncond + GUIDANCE * (noise_cond - noise_uncond)


def solution(mesh):
    in_specs = (
        P("cfg", "groups", ("blk", "ulysses"), None),
        P("cfg", "groups", ("blk", "ulysses"), None),
        P("cfg", "groups"),
        P("groups"),
        P(None, "groups", None),
        P(),
        P(None, ("blk", "ulysses", "cfg")),
        P(None, ("blk", "ulysses", "cfg")),
        P(None, None, ("ulysses", "cfg")),
        P(("ulysses", "cfg"), None),
        P("blk", ("ulysses", "cfg")),
        P(("ulysses", "cfg"), "blk"),
        P(),
        P(),
    )
    out_specs = P("groups", None, ("blk", "ulysses", "cfg"), None)
    return jax.shard_map(body, mesh=mesh, in_specs=in_specs, out_specs=out_specs, check_vma=False)
```

profile of v0, /device:TPU:0, one launch (start us, length us, event | category | flops | bytes accessed | tf_op | source)
XLA Modules:
  0.0 583.4 jit_solution(9271355319539368346)
XLA Ops:
  6.6 0.7 all-gather.10.cloned.1.call-update
  8.1 0.3 convolution_reduce_fusion
  8.4 0.6 dynamic-slice.1
  9.7 0.3 fusion.110
  10.0 0.2 dynamic-update-slice
  10.2 62.9 %all-reduce = f32[2432]{0:T(1024)S(1)} all-reduce(f32[2432]{0:T(1024)S(1)} %dynamic-update-slice), channel_id=2, replica_groups=mesh['groups'=2,'blk'=4,'ulysses'=2,'cfg'=2] {'blk','ulysses','cfg'}, use_global_device_ids=true, to_apply=%add | all-reduce | flops 2432 | bytes 19456
  73.2 5.2 convolution_bitcast_fusion
  78.3 17.7 %all-gather.2 = f32[16,1520,2]{1,2,0:T(2,128)S(1)} all-gather(f32[1,1520,2]{1,2,0:T(2,128)S(1)} %convolution_bitcast_fusion), channel_id=3, replica_groups=mesh['groups'=2,'blk'=4,'ulysses'=2,'cfg'=2] {'blk','ulysses','cfg'}, dimensions={0}, use_global_device_ids=true | all-gather | bytes 206720 | tf_op jit(solution)/shard_map/all_gather | solution.py:141
  96.0 0.3 reshape.1011
  96.3 0.3 dynamic-slice_reduce_fusion
  96.7 0.1 convert_reduce_fusion
  96.9 0.3 fusion.50
  97.1 0.3 slice_reduce_fusion.4
  97.4 0.2 fusion.53
  97.6 10.5 %all_gather.35 = bf16[1,128,2432]{2,1,0:T(8,128)(2,1)S(1)} all-gather(bf16[1,64,2432]{2,1,0:T(8,128)(2,1)S(1)} %fusion.53), channel_id=1, replica_groups=mesh['groups'=2,'blk'=4,'ulysses'=2,'cfg'=2] {'ulysses'}, dimensions={1}, use_global_device_ids=true | all-gather | bytes 933888 | tf_op jit(solution)/shard_map/all_gather | solution.py:151
  108.2 6.5 %fusion.21 = f32[3,1,128,1024]{3,2,0,1:T(8,128)S(1)} fusion(bf16[5,2432,1024]{2,1,0:T(8,128)(2,1)} %all-gather.10.cloned.1.call-done, bf16[1,128,2432]{2,1,0:T(8,128)(2,1)S(1)} %all_gather.35), kind=kOutput, calls=%fused_computation.26 | convolution fusion | flops 1912602624 | bytes 17137664 | tf_op jit(solution)/shard_map/prd,jdc->jprc/dot_general | solution.py:159
  114.7 0.2 copy.67
  115.0 1.0 copy.68
  116.0 2.0 slice_multiply_fusion.2
  118.0 0.9 pad_maximum_fusion
  118.9 0.7 all-gather.14.cloned.1.call-update
  119.7 0.2 fusion.77
  119.8 0.2 multiply_reduce_fusion.2
  120.1 0.1 add_convert_fusion.2
  120.9 4.9 all_gather.37
  125.8 5.3 fusion.32
  131.3 0.1 reduce_sum.126
  131.5 0.1 mul.478
  131.7 15.8 %all_gather.38 = bf16[2,1,48,1024]{3,0,1,2:T(2,128)(2,1)S(1)} all-gather(bf16[2,1,12,1024]{3,0,1,2:T(2,128)(2,1)S(1)} %copy.64), channel_id=1, replica_groups=mesh['groups'=2,'blk'=4,'ulysses'=2,'cfg'=2] {'blk'}, dimensions={2}, use_global_device_ids=true | all-gather | bytes 245760 | tf_op jit(solution)/shard_map/all_gather | solution.py:180
  147.4 0.8 slice_reduce_fusion
  148.3 0.2 reshape.995
  148.4 0.2 copy.61
  148.7 0.2 copy.60
  148.9 0.2 reshape.996
  149.1 0.3 select_reduce_fusion.1
  149.4 16.9 %all-gather.12.cloned.1.call-done = bf16[2,1,512,1024]{3,2,0,1:T(8,128)(2,1)} async-done(((bf16[2,1,128,1024]{3,2,0,1:T(8,128)(2,1)}), bf16[2,1,512,1024]{3,2,0,1:T(8,128)(2,1)}) %all-gather.12.cloned.1.call-update) | async-done | bytes 2097168 | tf_op jit(solution)/shard_map/all_gather | solution.py:186
  166.4 3.1 fusion.107
  169.4 1.5 copy.69
  170.9 2.3 copy.70
  173.2 0.9 select_reduce_fusion
  174.2 0.1 fusion.59
  174.3 1.1 fusion.5
  175.4 0.3 fusion.31
  175.7 1.1 fusion.38
  176.7 4.8 all-gather.14.cloned.1.call-done
  181.6 4.1 fusion.4
  185.8 0.5 all-gather.18.cloned.1.call-update
  186.4 0.5 all-gather.20.cloned.1.call-update
  186.9 15.8 %reduce-scatter.3.cloned.1.call-done = bf16[64,1,2432]{2,0,1:T(8,128)(2,1)} async-done(((bf16[128,1,2432]{2,0,1:T(8,128)(2,1)}), bf16[64,1,2432]{2,0,1:T(8,128)(2,1)}) %reduce-scatter.3.cloned.1.call-update) | async-done | bytes 311312 | tf_op jit(solution)/shard_map/reduce_scatter | solution.py:194
  202.8 1.2 fusion.58
  204.0 1.2 multiply_reduce_fusion.1
  205.2 1.9 add_convert_fusion.1
  207.1 0.3 reduce-scatter.5.cloned.1.call-start
  207.4 151.8 %all-gather.18.cloned.1.call-done = bf16[2432,1792]{1,0:T(8,128)(2,1)} async-done(((bf16[608,1792]{1,0:T(8,128)(2,1)}), bf16[2432,1792]{1,0:T(8,128)(2,1)}) %all-gather.18.cloned.1.call-update) | async-done | bytes 8716304 | tf_op jit(solution)/shard_map/all_gather | solution.py:211
  359.2 154.6 %all-gather.20.cloned.1.call-done = bf16[1792,2432]{0,1:T(8,128)(2,1)} async-done(((bf16[1792,608]{0,1:T(8,128)(2,1)}), bf16[1792,2432]{0,1:T(8,128)(2,1)}) %all-gather.20.cloned.1.call-update) | async-done | bytes 8716304 | tf_op jit(solution)/shard_map/all_gather | solution.py:215
  513.8 17.6 %all-gather.16.cloned.1.call-done = bf16[256,2432]{1,0:T(8,128)(2,1)} async-done(((bf16[64,2432]{1,0:T(8,128)(2,1)}), bf16[256,2432]{1,0:T(8,128)(2,1)}) %all-gather.16.cloned.1.call-update) | async-done | bytes 1245200 | tf_op jit(solution)/shard_map/all_gather | solution.py:207
  531.4 13.0 %convolution_convert_fusion = bf16[256,2432]{1,0:T(8,128)(2,1)} fusion(bf16[1792,2432]{0,1:T(8,128)(2,1)} %all-gather.20.cloned.1.call-done, bf16[256,2432]{1,0:T(8,128)(2,1)} %all-gather.16.cloned.1.call-done, bf16[2432,1792]{1,0:T(8,128)(2,1)} %all-gather.18.cloned.1.call-done), kind=kOutput, calls=%fused_computation.6 | convolution fusion | flops 4467490816 | bytes 19922944 | tf_op jit(solution)/shard_map/dot_general | solution.py:218
  544.4 26.2 %reduce-scatter.5.cloned.1.call-done = bf16[64,2432]{1,0:T(8,128)(2,1)} async-done(((bf16[256,2432]{1,0:T(8,128)(2,1)}), bf16[64,2432]{1,0:T(8,128)(2,1)}) %reduce-scatter.5.cloned.1.call-update) | async-done | bytes 311312 | tf_op jit(solution)/shard_map/reduce_scatter | solution.py:217
  570.6 1.2 fusion.105
  571.8 1.3 multiply_reduce_fusion
  573.1 1.4 convolution_bitcast_fusion.2
  574.5 0.1 copy.71
  574.8 1.1 collective-permute-done
  575.9 0.6 multiply_add_fusion.1
  (81 shorter events, 1.5 us)
Async XLA Ops:
  6.5 1.5 copy-start
  6.5 1.9 copy-start.11
  6.5 3.1 copy-start.6
  6.5 66.5 %copy-start.8 = (f32[2,1,2432]{2,1,0:T(1,128)S(1)}, f32[2,1,2432]{2,1,0:T(1,128)}, u32[]{:S(2)}) copy-start(f32[2,1,2432]{2,1,0:T(1,128)} %param.18) | copy-start | bytes 58372
  6.5 101.6 %all-gather.10.cloned.1.call-start = ((), (), s32[]{:S(2)}) async-start(), calls=%async_computation.2 | async-start | bytes 37355520 | tf_op jit(solution)/shard_map/all_gather | solution.py:157
  7.3 159.1 %all-gather.12.cloned.1.call-start = ((), (), s32[]{:S(2)}) async-start(), calls=%async_computation.3 | async-start | bytes 2621440 | tf_op jit(solution)/shard_map/all_gather | solution.py:186
  73.1 23.5 %copy-start.9 = (f32[3,64]{1,0:T(4,128)S(1)}, f32[3,64]{1,0:T(4,128)}, u32[]{:S(2)}) copy-start(f32[3,64]{1,0:T(4,128)} %param.26) | copy-start | bytes 2308
  73.1 23.6 %copy-start.2 = (bf16[1,1,64,2432]{3,2,1,0:T(8,128)(2,1)S(1)}, bf16[1,1,64,2432]{3,2,1,0:T(8,128)(2,1)}, u32[]{:S(2)}) copy-start(bf16[1,1,64,2432]{3,2,1,0:T(8,128)(2,1)} %param.14) | copy-start | bytes 933892
  115.0 4.7 copy-start.7
  118.9 62.7 %all-gather.14.cloned.1.call-start = ((), (), s32[]{:S(2)}) async-start(), calls=%async_computation.4 | async-start | bytes 7471104 | tf_op jit(solution)/shard_map/all_gather | solution.py:191
  119.6 83.2 %reduce-scatter.3.cloned.1.call-start = ((), (), s32[]{:S(2)}) async-start(), calls=%async_computation.5 | async-start | bytes 933888 | tf_op jit(solution)/shard_map/reduce_scatter | solution.py:194
  125.8 22.6 %copy-start.4 = (f32[1,1,128,1024]{3,2,0,1:T(8,128)S(1)}, f32[1,1,128,1024]{3,2,0,1:T(8,128)}, u32[]{:S(2)}) copy-start(f32[1,1,128,1024]{3,2,0,1:T(8,128)} %get-tuple-element.21) | copy-start | bytes 1572868
  174.1 1.5 copy-start.5
  185.7 173.5 %all-gather.18.cloned.1.call-start = ((), (), s32[]{:S(2)}) async-start(), calls=%async_computation.7 | async-start | bytes 10895360 | tf_op jit(solution)/shard_map/all_gather | solution.py:211
  186.3 327.5 %all-gather.20.cloned.1.call-start = ((), (), s32[]{:S(2)}) async-start(), calls=%async_computation.8 | async-start | bytes 10895360 | tf_op jit(solution)/shard_map/all_gather | solution.py:215
  186.9 344.5 %all-gather.16.cloned.1.call-start = ((), (), s32[]{:S(2)}) async-start(), calls=%async_computation.6 | async-start | bytes 1556480 | tf_op jit(solution)/shard_map/all_gather | solution.py:207
  207.1 363.5 %copy-start.3 = (bf16[64,1,2432]{2,0,1:T(8,128)(2,1)S(1)}, bf16[64,1,2432]{2,0,1:T(8,128)(2,1)}, u32[]{:S(2)}) copy-start(bf16[64,1,2432]{2,0,1:T(8,128)(2,1)} %reduce-scatter.3.cloned.1.call-done) | copy-start | bytes 933892
  207.1 366.0 %copy-start.10 = (bf16[2432,64]{0,1:T(8,128)(2,1)S(1)}, bf16[2432,64]{0,1:T(8,128)(2,1)}, u32[]{:S(2)}) copy-start(bf16[2432,64]{0,1:T(8,128)(2,1)} %param.27) | copy-start | bytes 933892
  207.1 363.4 %reduce-scatter.5.cloned.1.call-start = ((), (), s32[]{:S(2)}) async-start(), calls=%async_computation.9 | async-start | bytes 1556480 | tf_op jit(solution)/shard_map/reduce_scatter | solution.py:217
  531.4 45.1 %copy-start.1 = (bf16[256,2432]{1,0:T(8,128)(2,1)S(1)}, bf16[256,2432]{1,0:T(8,128)(2,1)}, u32[]{:S(2)}) copy-start(bf16[256,2432]{1,0:T(8,128)(2,1)} %param.19) | copy-start | bytes 3735556
  574.7 1.2 collective-permute-start
Sparse Core Ops, SparseCore 0:
  8.9 42.6 all-gather.9
  119.0 47.3 all-gather.11
  167.9 13.6 all-gather.13
  185.8 16.8 reduce-scatter.2
  204.2 154.9 all-gather.17
  360.6 153.1 all-gather.19
  515.4 15.9 all-gather.15
  544.5 26.0 reduce-scatter.4
where the time goes:
time: 584 us; the launch traced here: 583 us
  waiting for transfers between devices  391 us (67%)
  blocking collectives  112 us (19%)
  matrix products  38.7 us (7%)
  between operations  16 us (3%)
  other arithmetic  13.3 us (2%)
  local copies, waits for them, and re-layouts  11.8 us (2%)
    all_gather x1, waiting for transfers between devices, body(): reduce_full = lax.all_gather(reduce_weight, 'blk', axis=1, tiled=True)  155 us
    all_gather x1, waiting for transfers between devices, body(): lax.all_gather(expand_weight, 'blk', axis=0, tiled=True)  152 us
    unnamed x1, blocking collectives  62.9 us
    reduce_scatter x1, waiting for transfers between devices, body(): lax.psum_scatter(jnp.dot(segment, reduce_full, preferred_element_type=jnp...  26.2 us
    all_gather x1, blocking collectives, body(): lax.all_gather(mod_part, ('blk', 'ulysses', 'cfg'), axis=2, tiled=True)  17.7 us
    all_gather x1, waiting for transfers between devices, body(): lax.all_gather(feed_input, ('ulysses', 'cfg'), axis=0, tiled=True)  17.6 us
    all_gather x1, waiting for transfers between devices, body(): lax.all_gather(image_kv, 'blk', axis=2, tiled=True)  16.9 us
    reduce_scatter x1, waiting for transfers between devices, body(): lax.psum_scatter(jnp.einsum('rpc,cd->rpd', segment, out_gathered, preferr...  15.8 us
  transfers between devices with their start and end apart: 9, of which 8 were waited for; matrix products, arithmetic and copies ran while one was open for 5% of the time, Pallas kernels for 0%

commit v1 on v0

--- a/solution.py
+++ b/solution.py
@@ -1,3 +1,4 @@
+import functools
 import math
 import jax
 import jax.numpy as jnp
@@ -9,6 +10,29 @@
 RMS_EPS = 1e-06
 NEG_FILL = -1e30
 block_keys = 512
+
+
+def treat_roots_on(payload, chip_axis):
+    p_count = jax.lax.psum(1, axis_name=chip_axis)
+    vals = []
+    pp = 1
+    while pp < p_count:
+        vals.append((pp - 1, pp))
+        pp = pp + 1
+    block_last = vals + [(p_count - 1, 0)]
+    current_arr = payload
+    in_order = [current_arr]
+    src_i = 0
+    while src_i < p_count - 1:
+        current_arr = jax.lax.ppermute(current_arr, axis_name=chip_axis, perm=block_last)
+        in_order += [current_arr]
+        src_i = src_i + 1
+    n_now = jnp.concatenate([*reversed(in_order)], axis=1)
+    d_next = jax.lax.axis_index(chip_axis)
+    return jnp.roll(n_now, (d_next + 1) * current_arr.shape[1], 1)
+
+
+_pair_marks = functools.partial(treat_roots_on, chip_axis="blk")
 
 
 def from_partner(value, axis, stride):
@@ -212,7 +236,7 @@
         preferred_element_type=jnp.float32,
     )
     feed_hidden = jax.nn.gelu(pre_active, approximate=True).astype(jnp.bfloat16)
-    reduce_full = lax.all_gather(reduce_weight, "blk", axis=1, tiled=True)
+    reduce_full = _pair_marks(reduce_weight)
     segment = feed_hidden
     feed_out = lax.psum_scatter(
         jnp.dot(segment, reduce_full, preferred_element_type=jnp.float32).astype(jnp.bfloat16),

time: 584 us -> 552 us (0.945)
  waiting for transfers between devices: 391 us -> 265 us
  starting transfers between devices: 0.57 us -> 72.7 us
  local copies, waits for them, and re-layouts: 11.8 us -> 33.5 us
    ppermute x0 -> x3, waiting for transfers between devices: none -> 215 us  [treat_roots_on(): jax.lax.ppermute(current_arr, axis_name=chip_axis, perm=block_last)]
    all_gather x1 -> x0, waiting for transfers between devices: 155 us -> none  [body(): reduce_full = lax.all_gather(reduce_weight, 'blk', axis=1, tiled=True)]
    all_gather x1, waiting for transfers between devices: 152 us -> 0.01 us  [body(): lax.all_gather(expand_weight, 'blk', axis=0, tiled=True)]
    ppermute x0 -> x3, starting transfers between devices: none -> 72.2 us  [treat_roots_on(): jax.lax.ppermute(current_arr, axis_name=chip_axis, perm=block_last)]
    unnamed x31 -> x44, local copies, waits for them, and re-layouts: 1.48 us -> 21.8 us
    all_gather x1, waiting for transfers between devices: 17.6 us -> 0.01 us  [body(): lax.all_gather(feed_input, ('ulysses', 'cfg'), axis=0, tiled=True)]
    reduce_scatter x1, waiting for transfers between devices: 15.8 us -> 0.01 us  [body(): lax.psum_scatter(jnp.einsum('rpc,cd->rpd', segment, out_gathered, preferr...]
  transfers between devices with their start and end apart: 9 -> 11, of which waited for: 8 -> 7; matrix products, arithmetic and copies ran while one was open for 5% -> 9% of each run, Pallas kernels for 0% -> 0%
where the time goes in v1:
time: 552 us; the launch traced here: 551 us
  waiting for transfers between devices  265 us (48%)
  blocking collectives  112 us (20%)
  starting transfers between devices  72.7 us (13%)
  matrix products  38.7 us (7%)
  local copies, waits for them, and re-layouts  33.5 us (6%)
  between operations  16 us (3%)
  other arithmetic  13.3 us (2%)
    ppermute x3, waiting for transfers between devices, treat_roots_on(): jax.lax.ppermute(current_arr, axis_name=chip_axis, perm=block_last)  215 us
    ppermute x3, starting transfers between devices, treat_roots_on(): jax.lax.ppermute(current_arr, axis_name=chip_axis, perm=block_last)  72.2 us
    unnamed x1, blocking collectives  62.9 us
    reduce_scatter x1, waiting for transfers between devices, body(): lax.psum_scatter(jnp.dot(segment, reduce_full, preferred_element_type=jnp...  25.8 us
    unnamed x44, local copies, waits for them, and re-layouts  21.8 us
    all_gather x1, blocking collectives, body(): lax.all_gather(mod_part, ('blk', 'ulysses', 'cfg'), axis=2, tiled=True)  17.7 us
    all_gather x1, waiting for transfers between devices, body(): lax.all_gather(image_kv, 'blk', axis=2, tiled=True)  17.1 us
    all_gather x1, blocking collectives, body(): lax.all_gather(jnp.stack([txt_set[0], txt_set[1]]), 'blk', axis=2, tiled=...  15.7 us
  transfers between devices with their start and end apart: 11, of which 7 were waited for; matrix products, arithmetic and copies ran while one was open for 9% of the time, Pallas kernels for 0%

profile of v1, /device:TPU:0, one launch (start us, length us, event | category | flops | bytes accessed | tf_op | source)
XLA Modules:
  0.0 551.3 jit_solution(18010061782395105779)
XLA Ops:
  6.6 0.7 all-gather.9.cloned.1.call-update
  8.1 0.3 convolution_reduce_fusion
  8.4 0.6 dynamic-slice.1
  9.7 0.3 fusion.116
  10.2 62.9 %all-reduce = f32[2432]{0:T(1024)S(1)} all-reduce(f32[2432]{0:T(1024)S(1)} %dynamic-update-slice), channel_id=2, replica_groups=mesh['groups'=2,'blk'=4,'ulysses'=2,'cfg'=2] {'blk','ulysses','cfg'}, use_global_device_ids=true, to_apply=%add | all-reduce | flops 2432 | bytes 19456
  73.2 5.2 convolution_bitcast_fusion
  78.3 17.7 %all-gather.2 = f32[16,1520,2]{1,2,0:T(2,128)S(1)} all-gather(f32[1,1520,2]{1,2,0:T(2,128)S(1)} %convolution_bitcast_fusion), channel_id=3, replica_groups=mesh['groups'=2,'blk'=4,'ulysses'=2,'cfg'=2] {'blk','ulysses','cfg'}, dimensions={0}, use_global_device_ids=true | all-gather | bytes 206720 | tf_op jit(solution)/shard_map/all_gather | solution.py:165
  96.0 0.3 reshape.1011
  96.3 0.3 dynamic-slice_reduce_fusion
  96.9 0.3 fusion.55
  97.1 0.3 slice_reduce_fusion.4
  97.4 0.2 fusion.58
  97.6 10.5 %all_gather.32 = bf16[1,128,2432]{2,1,0:T(8,128)(2,1)S(1)} all-gather(bf16[1,64,2432]{2,1,0:T(8,128)(2,1)S(1)} %fusion.58), channel_id=1, replica_groups=mesh['groups'=2,'blk'=4,'ulysses'=2,'cfg'=2] {'ulysses'}, dimensions={1}, use_global_device_ids=true | all-gather | bytes 933888 | tf_op jit(solution)/shard_map/all_gather | solution.py:175
  108.2 6.5 %fusion.26 = f32[3,1,128,1024]{3,2,0,1:T(8,128)S(1)} fusion(bf16[5,2432,1024]{2,1,0:T(8,128)(2,1)} %all-gather.9.cloned.1.call-done, bf16[1,128,2432]{2,1,0:T(8,128)(2,1)S(1)} %all_gather.32), kind=kOutput, calls=%fused_computation.28 | convolution fusion | flops 1912602624 | bytes 17137664 | tf_op jit(solution)/shard_map/prd,jdc->jprc/dot_general | solution.py:183
  114.7 0.2 copy.67
  115.0 1.0 copy.68
  116.0 2.0 slice_multiply_fusion.2
  118.0 0.9 pad_maximum_fusion
  118.9 0.7 all-gather.13.cloned.1.call-update
  119.8 0.2 multiply_reduce_fusion.2
  120.9 4.8 all_gather.34
  125.8 0.2 copy.61
  126.1 0.2 copy.60
  126.3 5.2 fusion.37
  132.0 15.7 %all_gather.35 = bf16[2,1,48,1024]{3,0,1,2:T(2,128)(2,1)S(1)} all-gather(bf16[2,1,12,1024]{3,0,1,2:T(2,128)(2,1)S(1)} %copy.64), channel_id=1, replica_groups=mesh['groups'=2,'blk'=4,'ulysses'=2,'cfg'=2] {'blk'}, dimensions={2}, use_global_device_ids=true | all-gather | bytes 245760 | tf_op jit(solution)/shard_map/all_gather | solution.py:204
  147.7 0.8 slice_reduce_fusion
  148.9 0.3 select_reduce_fusion.1
  149.2 17.1 %all-gather.11.cloned.1.call-done = bf16[2,1,512,1024]{3,2,0,1:T(8,128)(2,1)} async-done(((bf16[2,1,128,1024]{3,2,0,1:T(8,128)(2,1)}), bf16[2,1,512,1024]{3,2,0,1:T(8,128)(2,1)}) %all-gather.11.cloned.1.call-update) | async-done | bytes 2097168 | tf_op jit(solution)/shard_map/all_gather | solution.py:210
  166.3 3.1 fusion.113
  169.4 1.5 copy.69
  170.9 2.3 copy.70
  173.2 0.9 select_reduce_fusion
  174.2 1.1 fusion.10
  175.3 0.3 fusion.36
  175.7 1.1 fusion.43
  176.7 4.8 all-gather.13.cloned.1.call-done
  181.5 4.1 fusion.9
  185.8 0.5 all-gather.17.cloned.1.call-update
  186.4 1.8 collective-permute-start
  188.2 70.3 %collective-permute-done = bf16[1792,608]{0,1:T(8,128)(2,1)S(1)} collective-permute-done((bf16[1792,608]{0,1:T(8,128)(2,1)}, bf16[1792,608]{0,1:T(8,128)(2,1)S(1)}, u32[]{:S(2)}, u32[]{:S(2)}) %collective-permute-start) | collective-permute-done | bytes 2179104 | tf_op jit(solution)/shard_map/ppermute | solution.py:27
  258.5 1.4 copy-done.4
  259.9 23.1 %collective-permute-start.1 = (bf16[1792,608]{0,1:T(8,128)(2,1)S(1)}, bf16[1792,608]{0,1:T(8,128)(2,1)}, u32[]{:S(2)}, u32[]{:S(2)}) collective-permute-start(bf16[1792,608]{0,1:T(8,128)(2,1)S(1)} %collective-permute-done), channel_id=1, source_target_pairs={{0,4},{4,8},{8,12},{12,0},{1,5},{5,9},{9,13},{13,1},{2,6},{6,10},{... | collective-permute-start | bytes 6537224 | tf_op jit(solution)/shard_map/ppermute | solution.py:27
  282.9 93.5 %collective-permute-done.1 = bf16[1792,608]{0,1:T(8,128)(2,1)} collective-permute-done((bf16[1792,608]{0,1:T(8,128)(2,1)S(1)}, bf16[1792,608]{0,1:T(8,128)(2,1)}, u32[]{:S(2)}, u32[]{:S(2)}) %collective-permute-start.1) | collective-permute-done | bytes 2179104 | tf_op jit(solution)/shard_map/ppermute | solution.py:27
  376.5 47.3 %collective-permute-start.2 = (bf16[1792,608]{0,1:T(8,128)(2,1)}, bf16[1792,608]{0,1:T(8,128)(2,1)}, u32[]{:S(2)}, u32[]{:S(2)}) collective-permute-start(bf16[1792,608]{0,1:T(8,128)(2,1)} %collective-permute-done.1), channel_id=1, source_target_pairs={{0,4},{4,8},{8,12},{12,0},{1,5},{5,9},{9,13},{13,1},{2,6},{6,10},{... | collective-permute-start | bytes 6537224 | tf_op jit(solution)/shard_map/ppermute | solution.py:27
  423.7 50.7 %collective-permute-done.2 = bf16[1792,608]{0,1:T(8,128)(2,1)} collective-permute-done((bf16[1792,608]{0,1:T(8,128)(2,1)}, bf16[1792,608]{0,1:T(8,128)(2,1)}, u32[]{:S(2)}, u32[]{:S(2)}) %collective-permute-start.2) | collective-permute-done | bytes 2179104 | tf_op jit(solution)/shard_map/ppermute | solution.py:27
  474.5 3.1 constant_dynamic-update-slice_fusion.7
  477.6 1.2 fusion.63
  478.8 1.2 multiply_reduce_fusion.1
  480.0 1.9 add_convert_fusion.1
  481.9 0.3 reduce-scatter.5.cloned.1.call-start
  482.2 3.2 constant_dynamic-update-slice_fusion.6
  485.5 3.1 constant_dynamic-update-slice_fusion.5
  488.6 1.5 constant_dynamic-update-slice_fusion.4
  490.1 3.3 constant_dynamic-update-slice_fusion.3
  493.4 3.1 constant_dynamic-update-slice_fusion.2
  496.6 1.5 constant_dynamic-update-slice_fusion.1
  498.1 1.5 constant_dynamic-update-slice_fusion
  499.5 13.1 %fusion.6 = bf16[256,2432]{1,0:T(8,128)(2,1)} fusion(bf16[1792,4864]{0,1:T(8,128)(2,1)} %constant_dynamic-update-slice_fusion, s32[]{:T(128)S(6)} %select_n.71, bf16[256,2432]{1,0:T(8,128)(2,1)} %all-gather.15.cloned.1.call-done, bf16[2432,1792]{1,0:T(8,128)(2,1)} %all-gather.17.cloned.1.call-done), kind=kOutput, calls=%fused_computation.8 | convolution fusion | flops 4467490816 | bytes 19922948 | tf_op jit(solution)/shard_map/dot_general | solution.py:242
  512.7 25.8 %reduce-scatter.5.cloned.1.call-done = bf16[64,2432]{1,0:T(8,128)(2,1)} async-done(((bf16[256,2432]{1,0:T(8,128)(2,1)}), bf16[64,2432]{1,0:T(8,128)(2,1)}) %reduce-scatter.5.cloned.1.call-update) | async-done | bytes 311312 | tf_op jit(solution)/shard_map/reduce_scatter | solution.py:241
  538.5 1.2 fusion.111
  539.7 1.3 multiply_reduce_fusion
  541.0 1.4 convolution_bitcast_fusion.2
  542.7 1.1 collective-permute-done.3
  543.8 0.6 multiply_add_fusion.1
  (98 shorter events, 2.8 us)
Async XLA Ops:
  6.5 1.5 copy-start
  6.5 1.9 copy-start.14
  6.5 3.1 copy-start.9
  6.5 66.5 %copy-start.11 = (f32[2,1,2432]{2,1,0:T(1,128)S(1)}, f32[2,1,2432]{2,1,0:T(1,128)}, u32[]{:S(2)}) copy-start(f32[2,1,2432]{2,1,0:T(1,128)} %param.18) | copy-start | bytes 58372
  6.5 101.6 %all-gather.9.cloned.1.call-start = ((), (), s32[]{:S(2)}) async-start(), calls=%async_computation.2 | async-start | bytes 37355520 | tf_op jit(solution)/shard_map/all_gather | solution.py:181
  7.3 159.1 %all-gather.11.cloned.1.call-start = ((), (), s32[]{:S(2)}) async-start(), calls=%async_computation.3 | async-start | bytes 2621440 | tf_op jit(solution)/shard_map/all_gather | solution.py:210
  73.1 23.5 %copy-start.12 = (f32[3,64]{1,0:T(4,128)S(1)}, f32[3,64]{1,0:T(4,128)}, u32[]{:S(2)}) copy-start(f32[3,64]{1,0:T(4,128)} %param.26) | copy-start | bytes 2308
  73.1 23.6 %copy-start.2 = (bf16[1,1,64,2432]{3,2,1,0:T(8,128)(2,1)S(1)}, bf16[1,1,64,2432]{3,2,1,0:T(8,128)(2,1)}, u32[]{:S(2)}) copy-start(bf16[1,1,64,2432]{3,2,1,0:T(8,128)(2,1)} %param.14) | copy-start | bytes 933892
  115.0 4.7 copy-start.10
  118.0 7.8 %copy-start.7 = (f32[1,1,128,1024]{3,2,0,1:T(8,128)S(1)}, f32[1,1,128,1024]{3,2,0,1:T(8,128)}, u32[]{:S(2)}) copy-start(f32[1,1,128,1024]{3,2,0,1:T(8,128)} %get-tuple-element.21) | copy-start | bytes 1572868
  118.9 62.7 %all-gather.13.cloned.1.call-start = ((), (), s32[]{:S(2)}) async-start(), calls=%async_computation.4 | async-start | bytes 7471104 | tf_op jit(solution)/shard_map/all_gather | solution.py:215
  119.6 358.0 %reduce-scatter.3.cloned.1.call-start = ((), (), s32[]{:S(2)}) async-start(), calls=%async_computation.5 | async-start | bytes 933888 | tf_op jit(solution)/shard_map/reduce_scatter | solution.py:218
  174.1 1.5 copy-start.8
  185.7 313.8 %all-gather.17.cloned.1.call-start = ((), (), s32[]{:S(2)}) async-start(), calls=%async_computation.7 | async-start | bytes 10895360 | tf_op jit(solution)/shard_map/all_gather | solution.py:235
  186.3 313.2 %all-gather.15.cloned.1.call-start = ((), (), s32[]{:S(2)}) async-start(), calls=%async_computation.6 | async-start | bytes 1556480 | tf_op jit(solution)/shard_map/all_gather | solution.py:231
  186.4 72.1 %collective-permute-start = (bf16[1792,608]{0,1:T(8,128)(2,1)}, bf16[1792,608]{0,1:T(8,128)(2,1)S(1)}, u32[]{:S(2)}, u32[]{:S(2)}) collective-permute-start(bf16[1792,608]{0,1:T(8,128)(2,1)} %param.25), channel_id=1, source_target_pairs={{0,4},{4,8},{8,12},{12,0},{1,5},{5,9},{9,13},{13,1},{2,6},{6,10},{... | collective-permute-start | bytes 6537224 | tf_op jit(solution)/shard_map/ppermute | solution.py:27
  258.5 1.4 copy-start.4
  259.9 116.6 %collective-permute-start.1 = (bf16[1792,608]{0,1:T(8,128)(2,1)S(1)}, bf16[1792,608]{0,1:T(8,128)(2,1)}, u32[]{:S(2)}, u32[]{:S(2)}) collective-permute-start(bf16[1792,608]{0,1:T(8,128)(2,1)S(1)} %collective-permute-done), channel_id=1, source_target_pairs={{0,4},{4,8},{8,12},{12,0},{1,5},{5,9},{9,13},{13,1},{2,6},{6,10},{... | collective-permute-start | bytes 6537224 | tf_op jit(solution)/shard_map/ppermute | solution.py:27
  376.5 98.0 %collective-permute-start.2 = (bf16[1792,608]{0,1:T(8,128)(2,1)}, bf16[1792,608]{0,1:T(8,128)(2,1)}, u32[]{:S(2)}, u32[]{:S(2)}) collective-permute-start(bf16[1792,608]{0,1:T(8,128)(2,1)} %collective-permute-done.1), channel_id=1, source_target_pairs={{0,4},{4,8},{8,12},{12,0},{1,5},{5,9},{9,13},{13,1},{2,6},{6,10},{... | collective-permute-start | bytes 6537224 | tf_op jit(solution)/shard_map/ppermute | solution.py:27
  481.9 56.6 %reduce-scatter.5.cloned.1.call-start = ((), (), s32[]{:S(2)}) async-start(), calls=%async_computation.8 | async-start | bytes 1556480 | tf_op jit(solution)/shard_map/reduce_scatter | solution.py:241
  482.2 6.4 %copy-start.3 = (bf16[1792,608]{0,1:T(8,128)(2,1)S(1)}, bf16[1792,608]{0,1:T(8,128)(2,1)}, u32[]{:S(2)}) copy-start(bf16[1792,608]{0,1:T(8,128)(2,1)} %param.25) | copy-start | bytes 6537220
  490.1 6.5 %copy-start.5 = (bf16[1792,608]{0,1:T(8,128)(2,1)S(1)}, bf16[1792,608]{0,1:T(8,128)(2,1)}, u32[]{:S(2)}) copy-start(bf16[1792,608]{0,1:T(8,128)(2,1)} %copy-done.4) | copy-start | bytes 6537220
  499.5 39.0 %copy-start.6 = (bf16[64,1,2432]{2,0,1:T(8,128)(2,1)S(1)}, bf16[64,1,2432]{2,0,1:T(8,128)(2,1)}, u32[]{:S(2)}) copy-start(bf16[64,1,2432]{2,0,1:T(8,128)(2,1)} %reduce-scatter.3.cloned.1.call-done) | copy-start | bytes 933892
  499.5 41.5 %copy-start.13 = (bf16[2432,64]{0,1:T(8,128)(2,1)S(1)}, bf16[2432,64]{0,1:T(8,128)(2,1)}, u32[]{:S(2)}) copy-start(bf16[2432,64]{0,1:T(8,128)(2,1)} %param.27) | copy-start | bytes 933892
  499.5 44.9 %copy-start.1 = (bf16[256,2432]{1,0:T(8,128)(2,1)S(1)}, bf16[256,2432]{1,0:T(8,128)(2,1)}, u32[]{:S(2)}) copy-start(bf16[256,2432]{1,0:T(8,128)(2,1)} %param.19) | copy-start | bytes 3735556
  542.6 1.2 collective-permute-start.3
Sparse Core Ops, SparseCore 0:
  8.9 42.6 all-gather.8
  119.0 47.3 all-gather.10
  167.9 13.6 all-gather.12
  185.8 16.8 reduce-scatter.2
  204.2 221.2 all-gather.16
  482.1 17.1 all-gather.14
  512.8 25.6 reduce-scatter.4
